TPU v7x, 32 devices: a whole 2x2x4 slice. The times are simulated.
32 devices in a mesh: shard: 16 (over z, y, core), model: 2 (over x).
Axes of the slice: x: 2, y: 2, z: 4, core: 2. Of those that a mesh axis runs over, the one named last changes fastest.
Arguments:
- gradients: float32 [128, 128, 4096], P(None, 'shard', 'model'), may hold values from -6 to 6
- momentum: float32 [128, 128, 4096], P(None, 'shard', 'model'), may hold values from -6 to 6
- weights: float32 [128, 128, 4096], P(None, 'shard', 'model'), may hold values from -0.1875 to 0.1875
Outputs:
- new_weights: float32 [128, 128, 4096], P(None, 'shard', 'model')
- new_momentum: float32 [128, 128, 4096], P(None, 'shard', 'model')
All inputs are finite; a program needn't handle non-finite values.
Results may differ from a plain program's by a relative error of at most 0.00012.
Values sent between devices are 32-bit elements; how exact they have to be, the bound alone decides.
A program may use at most 128 MiB of HBM per device.

v0:
```python
import jax
import jax.numpy as jnp
from jax import lax
from jax.sharding import PartitionSpec as P

ITERS = 4
hold_rate = 0.9
learn_rate = 0.8


def local(gradients, momentum, weights):
    new_momentum = hold_rate * momentum + gradients
    direction = hold_rate * new_momentum + gradients
    moved = lax.all_to_all(direction, "shard", split_axis=0, concat_axis=1, tiled=True)
    total = lax.psum(jnp.sum(moved * moved, axis=(1, 2), keepdims=True), "model")
    iterate = moved * lax.rsqrt(total + 1e-06)
    for step in range(ITERS):
        gram = lax.psum(
            jnp.einsum("mik,mjk->mij", iterate, iterate, precision=lax.Precision.HIGHEST), "model"
        )
        mixed = -4.775 * gram + 2.0315 * jnp.einsum(
            "mij,mjk->mik", gram, gram, precision=lax.Precision.HIGHEST
        )
        iterate = 3.4445 * iterate + jnp.einsum(
            "mij,mjk->mik", mixed, iterate, precision=lax.Precision.HIGHEST
        )
    back = lax.all_to_all(iterate, "shard", split_axis=1, concat_axis=0, tiled=True)
    new_weights = weights - learn_rate * back
    return (new_weights, new_momentum)


def solution(mesh):
    return jax.shard_map(
        local,
        mesh=mesh,
        in_specs=(P(None, "shard", "model"), P(None, "shard", "model"), P(None, "shard", "model")),
        out_specs=(P(None, "shard", "model"), P(None, "shard", "model")),
        check_vma=False,
    )
```

profile of v0, /device:TPU:1, one launch (start us, length us, event | category | flops | bytes accessed | tf_op | source)
XLA Modules:
  0.0 666.5 jit_solution(225198048523611833)
XLA Ops:
  7.2 0.0 all-reduce.5.cloned.1.call-start
  7.2 9.3 %multiply_add_fusion.4 = (f32[128,8,2048]{2,1,0:T(8,128)S(1)}, f32[128,8,2048]{2,1,0:T(8,128)}) fusion(f32[128,8,2048]{2,1,0:T(8,128)} %param.3, f32[128,8,2048]{2,1,0:T(8,128)} %param.4), kind=kLoop, calls=%fused_computation.8 | loop fusion | flops 8388608 | bytes 33554432 | tf_op jit(solution)/shard_map/add | solution.py:13
  16.5 189.7 %all_to_all.27 = f32[128,8,2048]{2,1,0:T(8,128)S(1)} all-to-all(f32[128,8,2048]{2,1,0:T(8,128)S(1)} %get-tuple-element.2), channel_id=1, replica_groups=mesh['shard'=16,'model'=2] {'shard'}, dimensions={0} | all-to-all | bytes 16777216 | tf_op jit(solution)/shard_map/all_to_all | solution.py:14
  206.2 0.0 copy-start
  206.2 3.4 copy-done
  209.5 0.8 fusion
  210.3 4.1 psum.35
  214.4 12.9 %fusion.2 = f32[8,128,128]{2,1,0:T(8,128)} fusion(f32[16,8,8,2048]{3,2,1,0:T(8,128)} %bitcast.44, f32[8]{0:T(128)S(1)} %rsqrt_bitcast_fusion), kind=kOutput, calls=%fused_computation.11 | convolution fusion | flops 3223322624 | bytes 8912928 | tf_op jit(solution)/shard_map/mik,mjk->mij/dot_general | solution.py:19
  227.3 0.0 all-reduce.5.cloned.1.call-update
  227.3 0.0 all-reduce.7.cloned.1.call-start
  227.4 29.3 %all-reduce.5.cloned.1.call-done = f32[8,128,128]{2,1,0:T(8,128)} async-done(((f32[8,128,128]{2,1,0:T(8,128)}), f32[8,128,128]{2,1,0:T(8,128)}) %all-reduce.5.cloned.1.call-update) | async-done | bytes 524304 | tf_op jit(solution)/shard_map/psum | solution.py:18
  256.7 2.1 fusion.8
  258.8 11.7 %multiply_add_fusion.3 = f32[8,128,2048]{2,1,0:T(8,128)S(1)} fusion(f32[16,8,8,2048]{3,2,1,0:T(8,128)} %bitcast.45, f32[8,128,128]{2,1,0:T(8,128)S(1)} %fusion.8, f32[8]{0:T(128)S(1)} %rsqrt_bitcast_fusion), kind=kOutput, calls=%fused_computation.7 | convolution fusion | flops 3229614080 | bytes 17301536 | tf_op jit(solution)/shard_map/mij,mjk->mik/dot_general | solution.py:24
  270.5 0.0 copy-start.1
  270.5 3.4 copy-done.1
  273.9 8.5 %fusion.9 = f32[8,128,128]{2,1,0:T(8,128)} fusion(f32[8,128,2048]{2,1,0:T(8,128)S(1)} %multiply_add_fusion.3), kind=kOutput, calls=%fused_computation.24 | convolution fusion | flops 3221225472 | bytes 8912896 | tf_op jit(solution)/shard_map/mik,mjk->mij/dot_general | solution.py:19
  282.4 0.0 all-reduce.7.cloned.1.call-update
  282.4 0.0 all-reduce.9.cloned.1.call-start
  282.5 28.8 %all-reduce.7.cloned.1.call-done = f32[8,128,128]{2,1,0:T(8,128)} async-done(((f32[8,128,128]{2,1,0:T(8,128)}), f32[8,128,128]{2,1,0:T(8,128)}) %all-reduce.7.cloned.1.call-update) | async-done | bytes 524304 | tf_op jit(solution)/shard_map/psum | solution.py:18
  311.3 2.1 fusion.7
  313.3 14.3 %multiply_add_fusion.2 = f32[8,128,2048]{2,1,0:T(8,128)S(1)} fusion(f32[8,128,2048]{2,1,0:T(8,128)} %copy-done.1, f32[8,128,128]{2,1,0:T(8,128)S(1)} %fusion.7), kind=kOutput, calls=%fused_computation.6 | convolution fusion | flops 3225419776 | bytes 17301504 | tf_op jit(solution)/shard_map/mij,mjk->mik/dot_general | solution.py:24
  327.7 0.0 copy-start.2
  327.7 3.4 copy-done.2
  331.1 8.5 %fusion.10 = f32[8,128,128]{2,1,0:T(8,128)} fusion(f32[8,128,2048]{2,1,0:T(8,128)S(1)} %multiply_add_fusion.2), kind=kOutput, calls=%fused_computation.25 | convolution fusion | flops 3221225472 | bytes 8912896 | tf_op jit(solution)/shard_map/mik,mjk->mij/dot_general | solution.py:19
  339.6 0.0 all-reduce.9.cloned.1.call-update
  339.6 0.0 all-reduce.11.cloned.1.call-start
  339.7 28.8 %all-reduce.9.cloned.1.call-done = f32[8,128,128]{2,1,0:T(8,128)} async-done(((f32[8,128,128]{2,1,0:T(8,128)}), f32[8,128,128]{2,1,0:T(8,128)}) %all-reduce.9.cloned.1.call-update) | async-done | bytes 524304 | tf_op jit(solution)/shard_map/psum | solution.py:18
  368.5 2.1 fusion.6
  370.5 14.1 %multiply_add_fusion.1 = f32[8,128,2048]{2,1,0:T(8,128)S(1)} fusion(f32[8,128,2048]{2,1,0:T(8,128)} %copy-done.2, f32[8,128,128]{2,1,0:T(8,128)S(1)} %fusion.6), kind=kOutput, calls=%fused_computation.5 | convolution fusion | flops 3225419776 | bytes 17301504 | tf_op jit(solution)/shard_map/mij,mjk->mik/dot_general | solution.py:24
  384.7 0.0 copy-start.3
  384.7 3.4 copy-done.3
  388.1 8.5 %fusion.11 = f32[8,128,128]{2,1,0:T(8,128)} fusion(f32[8,128,2048]{2,1,0:T(8,128)S(1)} %multiply_add_fusion.1), kind=kOutput, calls=%fused_computation.26 | convolution fusion | flops 3221225472 | bytes 8912896 | tf_op jit(solution)/shard_map/mik,mjk->mij/dot_general | solution.py:19
  396.6 0.0 all-reduce.11.cloned.1.call-update
  396.6 28.8 %all-reduce.11.cloned.1.call-done = f32[8,128,128]{2,1,0:T(8,128)} async-done(((f32[8,128,128]{2,1,0:T(8,128)}), f32[8,128,128]{2,1,0:T(8,128)}) %all-reduce.11.cloned.1.call-update) | async-done | bytes 524304 | tf_op jit(solution)/shard_map/psum | solution.py:18
  425.4 2.1 fusion.5
  427.5 14.9 %multiply_add_fusion = f32[8,128,2048]{2,1,0:T(8,128)S(1)} fusion(f32[8,128,2048]{2,1,0:T(8,128)} %copy-done.3, f32[8,128,128]{2,1,0:T(8,128)S(1)} %fusion.5), kind=kOutput, calls=%fused_computation.4 | convolution fusion | flops 3225419776 | bytes 17301504 | tf_op jit(solution)/shard_map/mij,mjk->mik/dot_general | solution.py:24
  442.4 4.9 copy.8
  447.2 188.9 %all_to_all.28 = f32[8,128,2048]{2,0,1:T(8,128)S(1)} all-to-all(f32[8,128,2048]{2,0,1:T(8,128)S(1)} %copy.8), channel_id=1, replica_groups=mesh['shard'=16,'model'=2] {'shard'}, dimensions={1} | all-to-all | bytes 16777216 | tf_op jit(solution)/shard_map/all_to_all | solution.py:27
  636.2 1.8 broadcast_multiply_fusion
  638.0 9.7 %copy.9 = f32[16,8,8,2048]{3,2,1,0:T(8,128)} copy(f32[16,8,8,2048]{3,1,2,0:T(8,128)S(1)} %bitcast.46) | data formatting | bytes 16777216 | tf_op jit(solution)/shard_map/mul | solution.py:28
  647.7 11.9 %bitcast_subtract_fusion = f32[128,8,2048]{2,1,0:T(8,128)} fusion(f32[128,8,2048]{2,1,0:T(8,128)} %param.5, f32[16,8,8,2048]{3,2,1,0:T(8,128)} %copy.9), kind=kLoop, calls=%fused_computation.1 | loop fusion | flops 2097152 | bytes 25165824 | tf_op jit(solution)/shard_map/sub | solution.py:28
  (1 shorter events, 0.0 us)
Async XLA Ops:
  7.2 249.5 %all-reduce.5.cloned.1.call-start = ((), (), s32[]{:S(2)}) async-start(), calls=%async_computation.2 | async-start | bytes 1048576 | tf_op jit(solution)/shard_map/psum | solution.py:18
  206.2 3.4 copy-start
  227.3 83.9 %all-reduce.7.cloned.1.call-start = ((), (), s32[]{:S(2)}) async-start(), calls=%async_computation.3 | async-start | bytes 1048576 | tf_op jit(solution)/shard_map/psum | solution.py:18
  270.5 3.4 copy-start.1
  282.4 86.0 %all-reduce.9.cloned.1.call-start = ((), (), s32[]{:S(2)}) async-start(), calls=%async_computation.4 | async-start | bytes 1048576 | tf_op jit(solution)/shard_map/psum | solution.py:18
  327.7 3.4 copy-start.2
  339.6 85.8 %all-reduce.11.cloned.1.call-start = ((), (), s32[]{:S(2)}) async-start(), calls=%async_computation.5 | async-start | bytes 1048576 | tf_op jit(solution)/shard_map/psum | solution.py:18
  384.7 3.4 copy-start.3
Sparse Core Ops, SparseCore 0:
  227.5 29.1 all-reduce.4
  282.6 28.6 all-reduce.6
  339.8 28.6 all-reduce.8
  396.7 28.6 all-reduce.10
where the time goes:
time: 675 us; the launch traced here: 667 us
  blocking collectives  383 us (57%)
  waiting for transfers between devices  116 us (17%)
  matrix products  102 us (15%)
  local copies, waits for them, and re-layouts  28.1 us (4%)
  other arithmetic  23.8 us (4%)
  between operations  14.3 us (2%)
    all_to_all x1, blocking collectives, local(): lax.all_to_all(direction, 'shard', split_axis=0, concat_axis=1, tiled=True)  190 us
    all_to_all x1, blocking collectives, local(): lax.all_to_all(iterate, 'shard', split_axis=1, concat_axis=0, tiled=True)  189 us
    psum x4, waiting for transfers between devices, local(): lax.psum(jnp.einsum('mik,mjk->mij', iterate, iterate, precision=lax.Preci...  116 us
    dot_general x4, matrix products, local(): jnp.einsum('mij,mjk->mik', mixed, iterate, precision=lax.Precision.HIGHEST)  55 us
    dot_general x4, matrix products, local(): jnp.einsum('mik,mjk->mij', iterate, iterate, precision=lax.Precision.HIGH...  38.5 us
    unnamed x8, local copies, waits for them, and re-layouts  13.6 us
  transfers between devices with their start and end apart: 4, of which 4 were waited for; matrix products, arithmetic and copies ran while one was open for 0% of the time, Pallas kernels for 0%

commit v1 on v0

--- a/solution.py
+++ b/solution.py
@@ -8,6 +8,11 @@
 learn_rate = 0.8
 
 
+def summed_here(value, mesh_axis):
+    parts = lax.all_gather(value, mesh_axis)
+    return jnp.sum(parts, axis=0)
+
+
 def local(gradients, momentum, weights):
     new_momentum = hold_rate * momentum + gradients
     direction = hold_rate * new_momentum + gradients
@@ -15,7 +20,7 @@
     total = lax.psum(jnp.sum(moved * moved, axis=(1, 2), keepdims=True), "model")
     iterate = moved * lax.rsqrt(total + 1e-06)
     for step in range(ITERS):
-        gram = lax.psum(
+        gram = summed_here(
             jnp.einsum("mik,mjk->mij", iterate, iterate, precision=lax.Precision.HIGHEST), "model"
         )
         mixed = -4.775 * gram + 2.0315 * jnp.einsum(

time: 675 us -> 645 us (0.956)
  waiting for transfers between devices: 116 us -> 86.2 us
    psum x4 -> x0, waiting for transfers between devices: 116 us -> none  [local(): lax.psum(jnp.einsum('mik,mjk->mij', iterate, iterate, precision=lax.Preci...]
    all_gather x0 -> x4, waiting for transfers between devices: none -> 86.2 us  [summed_here(): parts = lax.all_gather(value, mesh_axis)]
where the time goes in v1:
time: 645 us; the launch traced here: 637 us
  blocking collectives  383 us (59%)
  matrix products  96.2 us (15%)
  waiting for transfers between devices  86.2 us (13%)
  other arithmetic  29.1 us (5%)
  local copies, waits for them, and re-layouts  28.1 us (4%)
  between operations  14.3 us (2%)
    all_to_all x1, blocking collectives, local(): lax.all_to_all(direction, 'shard', split_axis=0, concat_axis=1, tiled=True)  190 us
    all_to_all x1, blocking collectives, local(): lax.all_to_all(iterate, 'shard', split_axis=1, concat_axis=0, tiled=True)  189 us
    all_gather x4, waiting for transfers between devices, summed_here(): parts = lax.all_gather(value, mesh_axis)  86.2 us
    dot_general x4, matrix products, local(): jnp.einsum('mij,mjk->mik', mixed, iterate, precision=lax.Precision.HIGHEST)  55 us
    dot_general x4, matrix products, local(): jnp.einsum('mik,mjk->mij', iterate, iterate, precision=lax.Precision.HIGH...  38.5 us
    unnamed x8, local copies, waits for them, and re-layouts  13.6 us
  transfers between devices with their start and end apart: 4, of which 4 were waited for; matrix products, arithmetic and copies ran while one was open for 0% of the time, Pallas kernels for 0%

profile of v1, /device:TPU:1, one launch (start us, length us, event | category | flops | bytes accessed | tf_op | source)
XLA Modules:
  0.0 636.8 jit_solution(3586302549167066661)
XLA Ops:
  7.2 0.0 all-gather.9.cloned.1.call-start
  7.2 9.3 %multiply_add_fusion.4 = (f32[128,8,2048]{2,1,0:T(8,128)S(1)}, f32[128,8,2048]{2,1,0:T(8,128)}) fusion(f32[128,8,2048]{2,1,0:T(8,128)} %param.3, f32[128,8,2048]{2,1,0:T(8,128)} %param.4), kind=kLoop, calls=%fused_computation.8 | loop fusion | flops 8388608 | bytes 33554432 | tf_op jit(solution)/shard_map/add | solution.py:18
  16.5 189.7 %all_to_all.27 = f32[128,8,2048]{2,1,0:T(8,128)S(1)} all-to-all(f32[128,8,2048]{2,1,0:T(8,128)S(1)} %get-tuple-element.2), channel_id=1, replica_groups=mesh['shard'=16,'model'=2] {'shard'}, dimensions={0} | all-to-all | bytes 16777216 | tf_op jit(solution)/shard_map/all_to_all | solution.py:19
  206.2 0.0 copy-start
  206.2 3.4 copy-done
  209.5 0.8 fusion
  210.3 4.1 psum.7
  214.4 12.9 %fusion.2 = f32[8,128,128]{2,1,0:T(8,128)} fusion(f32[16,8,8,2048]{3,2,1,0:T(8,128)} %bitcast.48, f32[8]{0:T(128)S(1)} %rsqrt_bitcast_fusion), kind=kOutput, calls=%fused_computation.11 | convolution fusion | flops 3223322624 | bytes 8912928 | tf_op jit(solution)/shard_map/mik,mjk->mij/dot_general | solution.py:24
  227.3 0.0 all-gather.9.cloned.1.call-update
  227.3 0.0 all-gather.11.cloned.1.call-start
  227.4 21.9 %all-gather.9.cloned.1.call-done = f32[16,128,128]{2,1,0:T(8,128)} async-done(((f32[8,128,128]{2,1,0:T(8,128)}), f32[16,128,128]{2,1,0:T(8,128)}) %all-gather.9.cloned.1.call-update) | async-done | bytes 1048592 | tf_op jit(solution)/shard_map/all_gather | solution.py:12
  249.3 1.3 reduce_sum.46
  250.7 0.7 fusion.8
  251.4 11.7 %multiply_add_fusion.3 = f32[8,128,2048]{2,1,0:T(8,128)S(1)} fusion(f32[16,8,8,2048]{3,2,1,0:T(8,128)} %bitcast.49, f32[8,128,128]{2,1,0:T(8,128)S(1)} %fusion.8, f32[8]{0:T(128)S(1)} %rsqrt_bitcast_fusion), kind=kOutput, calls=%fused_computation.7 | convolution fusion | flops 3229614080 | bytes 17301536 | tf_op jit(solution)/shard_map/mij,mjk->mik/dot_general | solution.py:29
  263.1 0.0 copy-start.1
  263.1 3.4 copy-done.1
  266.5 8.5 %fusion.9 = f32[8,128,128]{2,1,0:T(8,128)} fusion(f32[8,128,2048]{2,1,0:T(8,128)S(1)} %multiply_add_fusion.3), kind=kOutput, calls=%fused_computation.24 | convolution fusion | flops 3221225472 | bytes 8912896 | tf_op jit(solution)/shard_map/mik,mjk->mij/dot_general | solution.py:24
  275.0 0.0 all-gather.11.cloned.1.call-update
  275.0 0.0 all-gather.13.cloned.1.call-start
  275.1 21.4 %all-gather.11.cloned.1.call-done = f32[16,128,128]{2,1,0:T(8,128)} async-done(((f32[8,128,128]{2,1,0:T(8,128)}), f32[16,128,128]{2,1,0:T(8,128)}) %all-gather.11.cloned.1.call-update) | async-done | bytes 1048592 | tf_op jit(solution)/shard_map/all_gather | solution.py:12
  296.5 1.3 reduce_sum.47
  297.8 0.7 fusion.7
  298.5 14.3 %multiply_add_fusion.2 = f32[8,128,2048]{2,1,0:T(8,128)S(1)} fusion(f32[8,128,2048]{2,1,0:T(8,128)} %copy-done.1, f32[8,128,128]{2,1,0:T(8,128)S(1)} %fusion.7), kind=kOutput, calls=%fused_computation.6 | convolution fusion | flops 3225419776 | bytes 17301504 | tf_op jit(solution)/shard_map/mij,mjk->mik/dot_general | solution.py:29
  312.8 0.0 copy-start.2
  312.8 3.4 copy-done.2
  316.2 8.5 %fusion.10 = f32[8,128,128]{2,1,0:T(8,128)} fusion(f32[8,128,2048]{2,1,0:T(8,128)S(1)} %multiply_add_fusion.2), kind=kOutput, calls=%fused_computation.25 | convolution fusion | flops 3221225472 | bytes 8912896 | tf_op jit(solution)/shard_map/mik,mjk->mij/dot_general | solution.py:24
  324.8 0.0 all-gather.13.cloned.1.call-update
  324.8 0.0 all-gather.15.cloned.1.call-start
  324.8 21.4 %all-gather.13.cloned.1.call-done = f32[16,128,128]{2,1,0:T(8,128)} async-done(((f32[8,128,128]{2,1,0:T(8,128)}), f32[16,128,128]{2,1,0:T(8,128)}) %all-gather.13.cloned.1.call-update) | async-done | bytes 1048592 | tf_op jit(solution)/shard_map/all_gather | solution.py:12
  346.2 1.3 reduce_sum.48
  347.6 0.7 fusion.6
  348.2 14.1 %multiply_add_fusion.1 = f32[8,128,2048]{2,1,0:T(8,128)S(1)} fusion(f32[8,128,2048]{2,1,0:T(8,128)} %copy-done.2, f32[8,128,128]{2,1,0:T(8,128)S(1)} %fusion.6), kind=kOutput, calls=%fused_computation.5 | convolution fusion | flops 3225419776 | bytes 17301504 | tf_op jit(solution)/shard_map/mij,mjk->mik/dot_general | solution.py:29
  362.4 0.0 copy-start.3
  362.4 3.4 copy-done.3
  365.8 8.5 %fusion.11 = f32[8,128,128]{2,1,0:T(8,128)} fusion(f32[8,128,2048]{2,1,0:T(8,128)S(1)} %multiply_add_fusion.1), kind=kOutput, calls=%fused_computation.26 | convolution fusion | flops 3221225472 | bytes 8912896 | tf_op jit(solution)/shard_map/mik,mjk->mij/dot_general | solution.py:24
  374.3 0.0 all-gather.15.cloned.1.call-update
  374.3 21.4 %all-gather.15.cloned.1.call-done = f32[16,128,128]{2,1,0:T(8,128)} async-done(((f32[8,128,128]{2,1,0:T(8,128)}), f32[16,128,128]{2,1,0:T(8,128)}) %all-gather.15.cloned.1.call-update) | async-done | bytes 1048592 | tf_op jit(solution)/shard_map/all_gather | solution.py:12
  395.7 1.3 reduce_sum.49
  397.1 0.7 fusion.5
  397.8 14.9 %multiply_add_fusion = f32[8,128,2048]{2,1,0:T(8,128)S(1)} fusion(f32[8,128,2048]{2,1,0:T(8,128)} %copy-done.3, f32[8,128,128]{2,1,0:T(8,128)S(1)} %fusion.5), kind=kOutput, calls=%fused_computation.4 | convolution fusion | flops 3225419776 | bytes 17301504 | tf_op jit(solution)/shard_map/mij,mjk->mik/dot_general | solution.py:29
  412.6 4.9 copy.8
  417.5 188.9 %all_to_all.28 = f32[8,128,2048]{2,0,1:T(8,128)S(1)} all-to-all(f32[8,128,2048]{2,0,1:T(8,128)S(1)} %copy.8), channel_id=1, replica_groups=mesh['shard'=16,'model'=2] {'shard'}, dimensions={1} | all-to-all | bytes 16777216 | tf_op jit(solution)/shard_map/all_to_all | solution.py:32
  606.5 1.8 broadcast_multiply_fusion
  608.3 9.7 %copy.9 = f32[16,8,8,2048]{3,2,1,0:T(8,128)} copy(f32[16,8,8,2048]{3,1,2,0:T(8,128)S(1)} %bitcast.50) | data formatting | bytes 16777216 | tf_op jit(solution)/shard_map/mul | solution.py:33
  618.0 11.9 %bitcast_subtract_fusion = f32[128,8,2048]{2,1,0:T(8,128)} fusion(f32[128,8,2048]{2,1,0:T(8,128)} %param.5, f32[16,8,8,2048]{3,2,1,0:T(8,128)} %copy.9), kind=kLoop, calls=%fused_computation.1 | loop fusion | flops 2097152 | bytes 25165824 | tf_op jit(solution)/shard_map/sub | solution.py:33
  (1 shorter events, 0.0 us)
Async XLA Ops:
  7.2 242.2 %all-gather.9.cloned.1.call-start = ((), (), s32[]{:S(2)}) async-start(), calls=%async_computation.2 | async-start | bytes 1572864 | tf_op jit(solution)/shard_map/all_gather | solution.py:12
  206.2 3.4 copy-start
  227.3 69.1 %all-gather.11.cloned.1.call-start = ((), (), s32[]{:S(2)}) async-start(), calls=%async_computation.3 | async-start | bytes 1572864 | tf_op jit(solution)/shard_map/all_gather | solution.py:12
  263.1 3.4 copy-start.1
  275.0 71.2 %all-gather.13.cloned.1.call-start = ((), (), s32[]{:S(2)}) async-start(), calls=%async_computation.4 | async-start | bytes 1572864 | tf_op jit(solution)/shard_map/all_gather | solution.py:12
  312.8 3.4 copy-start.2
  324.8 71.0 %all-gather.15.cloned.1.call-start = ((), (), s32[]{:S(2)}) async-start(), calls=%async_computation.5 | async-start | bytes 1572864 | tf_op jit(solution)/shard_map/all_gather | solution.py:12
  362.4 3.4 copy-start.3
Sparse Core Ops, SparseCore 0:
  227.5 21.8 all-gather.8
  275.1 21.2 all-gather.10
  324.9 21.2 all-gather.12
  374.4 21.2 all-gather.14
